TPU v7x, 32 devices: a whole 2x2x4 slice. The times are simulated.
32 devices in a mesh: tp: 2 (over x), dp: 4 (over y, core), rep: 4 (over z).
Axes of the slice: x: 2, y: 2, z: 4, core: 2. Of those that a mesh axis runs over, the one named last changes fastest.
Arguments:
- prompts: bfloat16 [12288, 8192], P(('dp', 'rep'), 'tp'), may hold values from -6 to 6
- frozen_projection_weight: bfloat16 [2, 8192, 2048], P(None, ('dp', 'rep'), 'tp'), may hold values from -5 to 5
- lowrank_down_factor: bfloat16 [2, 8192, 64], P(None, ('dp', 'rep')), may hold values from -0.119628906 to 0.119628906
- lowrank_up_factor: bfloat16 [2, 64, 2048], P(None, None, 'tp'), may hold values from -0.59765625 to 0.59765625
- magnitude: float32 [2, 2048], P(None, 'tp'), may hold values from 0.5 to 2
Outputs:
- key_values: bfloat16 [2, 12288, 2048], P(None, ('dp', 'rep'), 'tp')
All inputs are finite; a program needn't handle non-finite values.
Results may differ from a plain program's by a relative error of at most 0.0049.
Values may be sent and summed in bfloat16 or wider, within the bound.
A program may use at most 128 MiB of HBM per device.

v0:
```python
import jax
import jax.numpy as jnp
from jax import lax
from jax.sharding import PartitionSpec as P

epsilon = 1e-06


def combine_weight_rows(weight_rows, down_rows, up_matrix):
    return weight_rows.astype(jnp.float32) + jnp.dot(
        down_rows, up_matrix, preferred_element_type=jnp.float32
    )


def prefilled_shard_values(
    frozen_projection_weight, lowrank_down_factor, lowrank_up_factor, magnitude, current_layer_index
):
    combined_weight = combine_weight_rows(
        frozen_projection_weight[current_layer_index],
        lowrank_down_factor[current_layer_index],
        lowrank_up_factor[current_layer_index],
    )
    squares = lax.psum(jnp.sum(combined_weight * combined_weight, axis=0), ("dp", "rep"))
    factor = magnitude[current_layer_index] / jnp.sqrt(squares + epsilon)
    return (combined_weight * factor).astype(jnp.bfloat16)


def local(prompts, frozen_projection_weight, lowrank_down_factor, lowrank_up_factor, magnitude):
    layer_total = frozen_projection_weight.shape[0]
    features = lax.all_gather(prompts, "tp", axis=1, tiled=True)
    outputs = []
    for current_layer_index in range(layer_total):
        prefilled_key_values = prefilled_shard_values(
            frozen_projection_weight,
            lowrank_down_factor,
            lowrank_up_factor,
            magnitude,
            current_layer_index,
        )
        result = jnp.dot(
            features,
            lax.all_gather(prefilled_key_values, ("dp", "rep"), axis=0, tiled=True),
            preferred_element_type=jnp.float32,
        )
        outputs.append(result.astype(jnp.bfloat16))
    return jnp.stack(outputs)


def solution(mesh):
    in_specs = (
        P(("dp", "rep"), "tp"),
        P(None, ("dp", "rep"), "tp"),
        P(None, ("dp", "rep"), None),
        P(None, None, "tp"),
        P(None, "tp"),
    )
    out_specs = P(None, ("dp", "rep"), "tp")
    return jax.shard_map(local, mesh=mesh, in_specs=in_specs, out_specs=out_specs, check_vma=False)
```

profile of v0, /device:TPU:0, one launch (start us, length us, event | category | flops | bytes accessed | tf_op | source)
XLA Modules:
  0.0 448.4 jit_solution(12562199270056117100)
XLA Ops:
  6.5 0.0 copy-start.2
  6.5 0.0 all-gather.6.cloned.1.call-start
  6.5 0.7 all-gather.6.cloned.1.call-update
  7.3 0.0 all-gather.4.cloned.1.call-start
  7.3 0.2 copy-done.2
  7.5 0.0 copy-done.3
  7.5 1.8 multiply_reduce_fusion
  9.4 0.1 copy-done
  9.4 1.8 multiply_reduce_fusion.1
  11.2 35.9 %all-reduce = (f32[1024]{0:T(1024)S(1)}, f32[1024]{0:T(1024)S(1)}) all-reduce(f32[1024]{0:T(1024)S(1)} %get-tuple-element.9, f32[1024]{0:T(1024)S(1)} %get-tuple-element.11), channel_id=1, replica_groups=mesh['tp'=2,'dp'=4,'rep'=4] {'dp','rep'}, use_global_device_ids=true, to_apply=%region_3.0 | all-reduce | flops 2048 | bytes 16384 | tf_op jit(solution)/shard_map/psum | solution.py:23
  47.2 0.0 copy-done.4
  47.2 2.8 multiply_convert_fusion.1
  50.0 0.0 all-gather.4.cloned.1.call-update
  50.1 0.0 all-gather.8.cloned.1.call-start
  50.1 1.2 multiply_convert_fusion
  51.4 0.0 all-gather.8.cloned.1.call-update
  51.4 112.8 %all-gather.6.cloned.1.call-done = bf16[768,8192]{1,0:T(8,128)(2,1)} async-done(((bf16[768,4096]{1,0:T(8,128)(2,1)}), bf16[768,8192]{1,0:T(8,128)(2,1)}) %all-gather.6.cloned.1.call-update) | async-done | bytes 12582928 | tf_op jit(solution)/shard_map/all_gather | solution.py:30
  164.1 128.7 %all-gather.4.cloned.1.call-done = bf16[8192,1024]{1,0:T(8,128)(2,1)} async-done(((bf16[512,1024]{1,0:T(8,128)(2,1)}), bf16[8192,1024]{1,0:T(8,128)(2,1)}) %all-gather.4.cloned.1.call-update) | async-done | bytes 16777232 | tf_op jit(solution)/shard_map/all_gather | solution.py:42
  292.8 20.0 %fusion = bf16[1,768,1024]{1,2,0:T(8,128)(2,1)} fusion(bf16[8192,1024]{1,0:T(8,128)(2,1)} %all-gather.4.cloned.1.call-done, bf16[768,8192]{1,0:T(8,128)(2,1)} %all-gather.6.cloned.1.call-done), kind=kOutput, calls=%fused_computation.9 | convolution fusion | flops 12885688320 | bytes 30932992 | tf_op jit(solution)/shard_map/dot_general | solution.py:40
  312.8 106.8 %all-gather.8.cloned.1.call-done = bf16[8192,1024]{1,0:T(8,128)(2,1)} async-done(((bf16[512,1024]{1,0:T(8,128)(2,1)}), bf16[8192,1024]{1,0:T(8,128)(2,1)}) %all-gather.8.cloned.1.call-update) | async-done | bytes 16777232 | tf_op jit(solution)/shard_map/all_gather | solution.py:42
  419.7 19.0 %fusion.1 = bf16[1,768,1024]{1,2,0:T(8,128)(2,1)S(1)} fusion(bf16[8192,1024]{1,0:T(8,128)(2,1)} %all-gather.8.cloned.1.call-done, bf16[768,8192]{1,0:T(8,128)(2,1)} %all-gather.6.cloned.1.call-done), kind=kOutput, calls=%fused_computation.10 | convolution fusion | flops 12885688320 | bytes 30932992 | tf_op jit(solution)/shard_map/dot_general | solution.py:40
  438.7 0.0 copy-done.1
  438.7 0.3 pad_maximum_fusion
  439.0 2.9 copy.6
  (7 shorter events, 0.0 us)
Async XLA Ops:
  6.5 0.9 copy-start.2
  6.5 1.0 copy-start.3
  6.5 157.6 %all-gather.6.cloned.1.call-start = ((), (), s32[]{:S(2)}) async-start(), calls=%async_computation.1 | async-start | bytes 18874368 | tf_op jit(solution)/shard_map/all_gather | solution.py:30
  7.3 285.6 %all-gather.4.cloned.1.call-start = ((), (), s32[]{:S(2)}) async-start(), calls=%async_computation | async-start | bytes 17825792 | tf_op jit(solution)/shard_map/all_gather | solution.py:42
  7.5 1.9 copy-start
  9.4 37.7 %copy-start.4 = (f32[2,1024]{1,0:T(2,128)S(1)}, f32[2,1024]{1,0:T(2,128)}, u32[]{:S(2)}) copy-start(f32[2,1024]{1,0:T(2,128)} %param.9) | copy-start | bytes 24580
  50.1 369.6 %all-gather.8.cloned.1.call-start = ((), (), s32[]{:S(2)}) async-start(), calls=%async_computation.2 | async-start | bytes 17825792 | tf_op jit(solution)/shard_map/all_gather | solution.py:42
  419.7 19.0 %copy-start.1 = (bf16[1,768,1024]{1,2,0:T(8,128)(2,1)S(1)}, bf16[1,768,1024]{1,2,0:T(8,128)(2,1)}, u32[]{:S(2)}) copy-start(bf16[1,768,1024]{1,2,0:T(8,128)(2,1)} %fusion) | copy-start | bytes 4718596
Sparse Core Ops, SparseCore 0:
  8.9 155.2 all-gather.5
  166.4 126.4 all-gather.3
  295.0 124.5 all-gather.7
where the time goes:
time: 449 us; the launch traced here: 448 us
  waiting for transfers between devices  349 us (78%)
  matrix products  42.7 us (10%)
  blocking collectives  35.9 us (8%)
  between operations  13.2 us (3%)
    all_gather x2, waiting for transfers between devices, local(): lax.all_gather(prefilled_key_values, ('dp', 'rep'), axis=0, tiled=True)  235 us
    all_gather x1, waiting for transfers between devices, local(): features = lax.all_gather(prompts, 'tp', axis=1, tiled=True)  113 us
    dot_general x2, matrix products, local(): jnp.dot(features, lax.all_gather(prefilled_key_values, ('dp', 'rep'), axi...  39 us
    psum x1, blocking collectives, prefilled_shard_values(): lax.psum(jnp.sum(combined_weight * combined_weight, axis=0), ('dp', 'rep'))  35.9 us
  transfers between devices with their start and end apart: 3, of which 3 were waited for; matrix products, arithmetic and copies ran while one was open for 6% of the time, Pallas kernels for 0%

commit v1 on v0

--- a/solution.py
+++ b/solution.py
@@ -27,7 +27,9 @@
 
 def local(prompts, frozen_projection_weight, lowrank_down_factor, lowrank_up_factor, magnitude):
     layer_total = frozen_projection_weight.shape[0]
-    features = lax.all_gather(prompts, "tp", axis=1, tiled=True)
+    features = jnp.concatenate(
+        lax.all_to_all(jnp.stack([prompts] * lax.axis_size("tp")), "tp", 0, 0), axis=1
+    )
     outputs = []
     for current_layer_index in range(layer_total):
         prefilled_key_values = prefilled_shard_values(

time: 449 us -> 327 us (0.73)
  waiting for transfers between devices: 349 us -> 76 us
  blocking collectives: 35.9 us -> 176 us
  other arithmetic: 4.38 us -> 12.7 us
  local copies, waits for them, and re-layouts: 3.15 us -> 8.75 us
    all_gather x2, waiting for transfers between devices: 235 us -> 76 us  [local(): lax.all_gather(prefilled_key_values, ('dp', 'rep'), axis=0, tiled=True)]
    all_to_all x0 -> x1, blocking collectives: none -> 140 us  [local(): lax.all_to_all(jnp.stack([prompts] * lax.axis_size('tp')), 'tp', 0, 0)]
    all_gather x1 -> x0, waiting for transfers between devices: 113 us -> none  [local(): features = lax.all_gather(prompts, 'tp', axis=1, tiled=True)]
    unnamed x10 -> x9, local copies, waits for them, and re-layouts: 0.27 us -> 8.75 us
    another operation x0 -> x1, other arithmetic: none -> 6.67 us  [local(): jnp.stack([prompts] * lax.axis_size('tp'))]
  transfers between devices with their start and end apart: 3 -> 2, of which waited for: 3 -> 1; matrix products, arithmetic and copies ran while one was open for 6% -> 11% of each run, Pallas kernels for 0% -> 0%
where the time goes in v1:
time: 327 us
  blocking collectives  176 us (54%)
  waiting for transfers between devices  76 us (23%)
  matrix products  40.3 us (12%)
  between operations  13.5 us (4%)
  other arithmetic  12.7 us (4%)
  local copies, waits for them, and re-layouts  8.75 us (3%)
    all_to_all x1, blocking collectives, local(): lax.all_to_all(jnp.stack([prompts] * lax.axis_size('tp')), 'tp', 0, 0)  140 us
    all_gather x2, waiting for transfers between devices, local(): lax.all_gather(prefilled_key_values, ('dp', 'rep'), axis=0, tiled=True)  76 us
    dot_general x2, matrix products, local(): jnp.dot(features, lax.all_gather(prefilled_key_values, ('dp', 'rep'), axi...  36.5 us
    psum x1, blocking collectives, prefilled_shard_values(): lax.psum(jnp.sum(combined_weight * combined_weight, axis=0), ('dp', 'rep'))  36 us
    unnamed x9, local copies, waits for them, and re-layouts  8.75 us
    another operation x1, other arithmetic, local(): jnp.stack([prompts] * lax.axis_size('tp'))  6.67 us
  transfers between devices with their start and end apart: 2, of which 1 were waited for; matrix products, arithmetic and copies ran while one was open for 11% of the time, Pallas kernels for 0%

profile of v1, /device:TPU:0, one launch (start us, length us, event | category | flops | bytes accessed | tf_op | source)
XLA Modules:
  0.0 326.8 jit_solution(6724172361121895028)
XLA Ops:
  6.5 0.0 copy-start.1
  6.5 0.0 copy-start.2
  6.5 0.0 all-gather.5.cloned.1.call-start
  6.5 0.0 copy-start
  6.5 3.3 multiply_reduce_fusion
  9.8 0.0 copy-done.1
  9.8 0.0 copy-done.2
  9.8 0.0 copy-done
  9.8 0.5 multiply_reduce_fusion.1
  10.3 0.0 copy-done.3
  10.3 36.0 %all-reduce = (f32[1024]{0:T(1024)S(1)}, f32[1024]{0:T(1024)S(1)}) all-reduce(f32[1024]{0:T(1024)S(1)} %get-tuple-element.9, f32[1024]{0:T(1024)S(1)} %get-tuple-element.11), channel_id=1, replica_groups=mesh['tp'=2,'dp'=4,'rep'=4] {'dp','rep'}, use_global_device_ids=true, to_apply=%region_3.0 | all-reduce | flops 2048 | bytes 16384 | tf_op jit(solution)/shard_map/psum | solution.py:23
  46.3 2.8 multiply_convert_fusion
  49.1 0.0 all-gather.5.cloned.1.call-update
  49.2 0.0 all-gather.3.cloned.1.call-start
  49.2 1.2 multiply_convert_fusion.1
  50.5 0.0 all-gather.3.cloned.1.call-update
  50.5 8.7 %copy.6 = bf16[768,4096]{0,1:T(8,128)(2,1)} copy(bf16[768,4096]{1,0:T(8,128)(2,1)} %param.5) | data formatting | bytes 12582912 | tf_op args[0]
  59.2 6.7 %pad_maximum_fusion = bf16[2,768,4096]{1,2,0:T(8,128)(2,1)S(1)} fusion(bf16[1,768,4096]{1,2,0:T(8,128)(2,1)} %bitcast.40), kind=kLoop, calls=%fused_computation | loop fusion | flops 6291456 | bytes 18874368 | tf_op jit(solution)/shard_map/stack | solution.py:31
  65.9 139.6 %all_to_all.5 = bf16[2,768,4096]{1,2,0:T(8,128)(2,1)} all-to-all(bf16[2,768,4096]{1,2,0:T(8,128)(2,1)S(1)} %pad_maximum_fusion), channel_id=1, replica_groups=mesh['tp'=2,'dp'=4,'rep'=4] {'tp'}, dimensions={0} | all-to-all | bytes 25165824 | tf_op jit(solution)/shard_map/all_to_all | solution.py:31
  205.5 0.0 all-gather.5.cloned.1.call-done
  205.5 18.3 %fusion.1 = bf16[1,768,1024]{2,1,0:T(8,128)(2,1)S(1)} fusion(bf16[768,8192]{0,1:T(8,128)(2,1)} %bitcast.41, bf16[8192,1024]{1,0:T(8,128)(2,1)} %all-gather.5.cloned.1.call-done), kind=kOutput, calls=%fused_computation.11 | convolution fusion | flops 12885688320 | bytes 30932992 | tf_op jit(solution)/shard_map/dot_general | solution.py:42
  223.8 76.0 %all-gather.3.cloned.1.call-done = bf16[8192,1024]{1,0:T(8,128)(2,1)} async-done(((bf16[512,1024]{1,0:T(8,128)(2,1)}), bf16[8192,1024]{1,0:T(8,128)(2,1)}) %all-gather.3.cloned.1.call-update) | async-done | bytes 16777232 | tf_op jit(solution)/shard_map/all_gather | solution.py:44
  299.7 18.2 %fusion = bf16[1,768,1024]{2,1,0:T(8,128)(2,1)S(1)} fusion(bf16[768,8192]{0,1:T(8,128)(2,1)} %bitcast.42, bf16[8192,1024]{1,0:T(8,128)(2,1)} %all-gather.3.cloned.1.call-done), kind=kOutput, calls=%fused_computation.10 | convolution fusion | flops 12885688320 | bytes 30932992 | tf_op jit(solution)/shard_map/dot_general | solution.py:42
  318.0 1.9 pad_maximum_fusion.1
  (4 shorter events, 0.0 us)
Async XLA Ops:
  6.5 3.3 %copy-start.1 = (bf16[2,64,1024]{2,1,0:T(8,128)(2,1)S(1)}, bf16[2,64,1024]{2,1,0:T(8,128)(2,1)}, u32[]{:S(2)}) copy-start(bf16[2,64,1024]{2,1,0:T(8,128)(2,1)} %param.8) | copy-start | bytes 786436
  6.5 3.3 %copy-start.2 = (bf16[2,512,64]{1,2,0:T(8,128)(2,1)S(1)}, bf16[2,512,64]{1,2,0:T(8,128)(2,1)}, u32[]{:S(2)}) copy-start(bf16[2,512,64]{1,2,0:T(8,128)(2,1)} %param.7) | copy-start | bytes 393220
  6.5 3.8 %copy-start.3 = (f32[2,1024]{1,0:T(2,128)S(1)}, f32[2,1024]{1,0:T(2,128)}, u32[]{:S(2)}) copy-start(f32[2,1024]{1,0:T(2,128)} %param.9) | copy-start | bytes 24580
  6.5 199.0 %all-gather.5.cloned.1.call-start = ((), (), s32[]{:S(2)}) async-start(), calls=%async_computation.2 | async-start | bytes 17825792 | tf_op jit(solution)/shard_map/all_gather | solution.py:44
  6.5 3.3 %copy-start = (bf16[2,512,1024]{2,1,0:T(8,128)(2,1)S(1)}, bf16[2,512,1024]{2,1,0:T(8,128)(2,1)}, u32[]{:S(2)}) copy-start(bf16[2,512,1024]{2,1,0:T(8,128)(2,1)} %param.6) | copy-start | bytes 6291460
  49.2 250.6 %all-gather.3.cloned.1.call-start = ((), (), s32[]{:S(2)}) async-start(), calls=%async_computation.1 | async-start | bytes 17825792 | tf_op jit(solution)/shard_map/all_gather | solution.py:44
Sparse Core Ops, SparseCore 0:
  49.3 123.5 all-gather.4
  175.1 124.5 all-gather.2

commit v2 on v0

--- a/solution.py
+++ b/solution.py
@@ -39,7 +39,15 @@
         )
         result = jnp.dot(
             features,
-            lax.all_gather(prefilled_key_values, ("dp", "rep"), axis=0, tiled=True),
+            jnp.concatenate(
+                lax.all_to_all(
+                    jnp.stack([prefilled_key_values] * lax.axis_size(("dp", "rep"))),
+                    ("dp", "rep"),
+                    0,
+                    0,
+                ),
+                axis=0,
+            ),
             preferred_element_type=jnp.float32,
         )
         outputs.append(result.astype(jnp.bfloat16))

time: 449 us -> 828 us (1.84)
  waiting for transfers between devices: 349 us -> 708 us
  local copies, waits for them, and re-layouts: 3.15 us -> 14.8 us
  starting transfers between devices: 0.08 us -> 10.3 us
    all_to_all x0 -> x2, waiting for transfers between devices: none -> 552 us  [local(): lax.all_to_all(jnp.stack([prefilled_key_values] * lax.axis_size(('dp', 'r...]
    all_gather x2 -> x0, waiting for transfers between devices: 235 us -> none  [local(): lax.all_gather(prefilled_key_values, ('dp', 'rep'), axis=0, tiled=True)]
    all_gather x1, waiting for transfers between devices: 113 us -> 155 us  [local(): features = lax.all_gather(prompts, 'tp', axis=1, tiled=True)]
    another operation x0 -> x2, local copies, waits for them, and re-layouts: none -> 11.9 us  [local(): jnp.stack([prefilled_key_values] * lax.axis_size(('dp', 'rep')))]
    all_to_all x0 -> x2, starting transfers between devices: none -> 10.3 us  [local(): lax.all_to_all(jnp.stack([prefilled_key_values] * lax.axis_size(('dp', 'r...]
  transfers between devices with their start and end apart: 3 -> 3, of which waited for: 3 -> 3; matrix products, arithmetic and copies ran while one was open for 6% -> 2% of each run, Pallas kernels for 0% -> 0%
where the time goes in v2:
time: 828 us; the launch traced here: 827 us
  waiting for transfers between devices  708 us (86%)
  matrix products  42.8 us (5%)
  blocking collectives  36 us (4%)
  local copies, waits for them, and re-layouts  14.8 us (2%)
  between operations  13.5 us (2%)
  starting transfers between devices  10.3 us (1%)
    all_to_all x2, waiting for transfers between devices, local(): lax.all_to_all(jnp.stack([prefilled_key_values] * lax.axis_size(('dp', 'r...  552 us
    all_gather x1, waiting for transfers between devices, local(): features = lax.all_gather(prompts, 'tp', axis=1, tiled=True)  155 us
    dot_general x2, matrix products, local(): jnp.dot(features, jnp.concatenate(lax.all_to_all(jnp.stack([prefilled_key...  39 us
    psum x1, blocking collectives, prefilled_shard_values(): lax.psum(jnp.sum(combined_weight * combined_weight, axis=0), ('dp', 'rep'))  36 us
  transfers between devices with their start and end apart: 3, of which 3 were waited for; matrix products, arithmetic and copies ran while one was open for 2% of the time, Pallas kernels for 0%

profile of v2, /device:TPU:0, one launch (start us, length us, event | category | flops | bytes accessed | tf_op | source)
XLA Modules:
  0.0 827.3 jit_solution(9007918507034801088)
XLA Ops:
  6.5 0.0 copy-start.2
  6.5 3.3 multiply_reduce_fusion
  9.8 0.0 copy-done.2
  9.8 0.0 copy-done.3
  9.8 0.0 copy-done
  9.8 0.5 multiply_reduce_fusion.1
  10.3 0.0 copy-done.4
  10.3 36.0 %all-reduce = (f32[1024]{0:T(1024)S(1)}, f32[1024]{0:T(1024)S(1)}) all-reduce(f32[1024]{0:T(1024)S(1)} %get-tuple-element.9, f32[1024]{0:T(1024)S(1)} %get-tuple-element.11), channel_id=1, replica_groups=mesh['tp'=2,'dp'=4,'rep'=4] {'dp','rep'}, use_global_device_ids=true, to_apply=%region_3.0 | all-reduce | flops 2048 | bytes 16384 | tf_op jit(solution)/shard_map/psum | solution.py:23
  46.3 1.8 multiply_convert_fusion
  48.2 6.0 stack.12
  54.2 5.1 all-to-all-start.1
  59.3 0.2 multiply_convert_fusion.1
  59.6 363.7 %all-to-all-done.1 = bf16[16,512,1024]{2,1,0:T(8,128)(2,1)} async-done(((bf16[16,512,1024]{2,1,0:T(8,128)(2,1)}), bf16[16,512,1024]{2,1,0:T(8,128)(2,1)}, u32[]{:S(2)}, u32[]{:S(2)}) %all-to-all-start.1) | async-done | bytes 16777248 | tf_op jit(solution)/shard_map/all_to_all | solution.py:43
  423.2 5.9 stack.10
  429.2 5.1 all-to-all-start
  434.3 0.0 all-gather.2.cloned.1.call-start
  434.4 0.7 all-gather.2.cloned.1.call-update
  435.1 155.2 %all-gather.2.cloned.1.call-done = bf16[768,8192]{1,0:T(8,128)(2,1)} async-done(((bf16[768,4096]{1,0:T(8,128)(2,1)}), bf16[768,8192]{1,0:T(8,128)(2,1)}) %all-gather.2.cloned.1.call-update) | async-done | bytes 12582928 | tf_op jit(solution)/shard_map/all_gather | solution.py:30
  590.3 20.0 %fusion.1 = bf16[1,768,1024]{1,2,0:T(8,128)(2,1)} fusion(bf16[8192,1024]{1,0:T(8,128)(2,1)} %bitcast.11, bf16[768,8192]{1,0:T(8,128)(2,1)} %all-gather.2.cloned.1.call-done), kind=kOutput, calls=%fused_computation.10 | convolution fusion | flops 12885688320 | bytes 30932992 | tf_op jit(solution)/shard_map/dot_general | solution.py:40
  610.3 188.0 %all-to-all-done = bf16[16,512,1024]{2,1,0:T(8,128)(2,1)} async-done(((bf16[16,512,1024]{2,1,0:T(8,128)(2,1)}), bf16[16,512,1024]{2,1,0:T(8,128)(2,1)}, u32[]{:S(2)}, u32[]{:S(2)}) %all-to-all-start) | async-done | bytes 16777248 | tf_op jit(solution)/shard_map/all_to_all | solution.py:43
  798.3 19.0 %fusion = bf16[1,768,1024]{1,2,0:T(8,128)(2,1)S(1)} fusion(bf16[8192,1024]{1,0:T(8,128)(2,1)} %bitcast.4, bf16[768,8192]{1,0:T(8,128)(2,1)} %all-gather.2.cloned.1.call-done), kind=kOutput, calls=%fused_computation.9 | convolution fusion | flops 12885688320 | bytes 30932992 | tf_op jit(solution)/shard_map/dot_general | solution.py:40
  817.3 0.0 copy-done.1
  817.3 0.3 pad_maximum_fusion
  817.6 2.9 copy.6
  (6 shorter events, 0.0 us)
Async XLA Ops:
  6.5 3.3 copy-start.2
  6.5 3.3 copy-start.3
  6.5 3.3 copy-start
  6.5 3.7 copy-start.4
  54.2 369.1 %all-to-all-start.1 = ((bf16[16,512,1024]{2,1,0:T(8,128)(2,1)}), bf16[16,512,1024]{2,1,0:T(8,128)(2,1)}, u32[]{:S(2)}, u32[]{:S(2)}) async-start(bf16[16,512,1024]{2,1,0:T(8,128)(2,1)} %stack.12), calls=%async_computation.1 | async-start | bytes 33554432 | tf_op jit(solution)/shard_map/all_to_all | solution.py:43
  429.2 369.1 %all-to-all-start = ((bf16[16,512,1024]{2,1,0:T(8,128)(2,1)}), bf16[16,512,1024]{2,1,0:T(8,128)(2,1)}, u32[]{:S(2)}, u32[]{:S(2)}) async-start(bf16[16,512,1024]{2,1,0:T(8,128)(2,1)} %stack.10), calls=%async_computation | async-start | bytes 33554432 | tf_op jit(solution)/shard_map/all_to_all | solution.py:43
  434.3 155.9 %all-gather.2.cloned.1.call-start = ((), (), s32[]{:S(2)}) async-start(), calls=%async_computation.2 | async-start | bytes 18874368 | tf_op jit(solution)/shard_map/all_gather | solution.py:30
  798.3 19.0 %copy-start.1 = (bf16[1,768,1024]{1,2,0:T(8,128)(2,1)S(1)}, bf16[1,768,1024]{1,2,0:T(8,128)(2,1)}, u32[]{:S(2)}) copy-start(bf16[1,768,1024]{1,2,0:T(8,128)(2,1)} %fusion.1) | copy-start | bytes 4718596
Sparse Core Ops, SparseCore 0:
  436.7 153.5 all-gather.1
